TPU v7x, 256 devices: a whole 4x4x8 slice. The times are simulated.
256 devices in a mesh: dp: 16 (over x, y_hi, core), pencil: 16 (over z, y_lo).
Axes of the slice: x: 4, y: 4 (y_hi: 2, y_lo: 2; y = y_hi * 2 + y_lo), z: 8, core: 2. Of those that a mesh axis runs over, the one named last changes fastest.
Arguments:
- field: bfloat16 [16, 64, 64, 64, 128], P('dp', 'pencil'), may hold values from -6 to 6
- cotangent: bfloat16 [16, 64, 64, 64, 128], P('dp', 'pencil'), may hold values from -6 to 6
- w_spec: bfloat16 [16, 16, 16, 64, 128], P('dp', 'pencil'), may hold values from -6 to 6
- w_local: bfloat16 [64, 64], replicated, may hold values from -0.75 to 0.75
Outputs:
- grad_field: bfloat16 [16, 64, 64, 64, 128], P('dp', 'pencil')
- grad_w: float32 [16, 16, 16, 64, 128], P('dp', 'pencil')
All inputs are finite; a program needn't handle non-finite values.
Results may differ from a plain program's by a relative error of at most 0.02.
Values may be sent and summed in bfloat16 or wider, within the bound.
A program may use at most 128 MiB of HBM per device.

v0:
```python
import math
import jax
import jax.numpy as jnp
from jax import lax
from jax.sharding import PartitionSpec as P

NX = 64
NY = 64
NZ = 128
CH = 64
MX = 16
MY = 16
MZ = 16


def phase_pair(length, mode_count, signed):
    position = jnp.arange(length, dtype=jnp.int32)
    indices = jnp.arange(mode_count, dtype=jnp.int32)
    frequency = (
        jnp.where(indices < mode_count // 2, indices, indices - mode_count) if signed else indices
    )
    product = jnp.mod(position[:, None] * frequency[None, :], length).astype(jnp.float32)
    angles = product * (2.0 * math.pi / length)
    return (jnp.cos(angles), jnp.sin(angles))


def grid_tables():
    cos_x, sin_x = phase_pair(NX, MX, True)
    cos_y, sin_y = phase_pair(NY, MY, True)
    cos_z, sin_z = phase_pair(NZ, MZ, False)
    forward_z = jnp.concatenate([cos_z, -sin_z], 1).astype(jnp.bfloat16)
    weight_z = jnp.where(jnp.arange(MZ, dtype=jnp.int32) == 0, 1.0, 2.0).astype(jnp.float32) / (
        NX * NY * NZ
    )
    inverse_z = jnp.concatenate([cos_z * weight_z, -sin_z * weight_z], 1).T
    adjoint_z = jnp.concatenate([cos_z, -sin_z], 1).T
    spectrum_scale = jnp.concatenate([weight_z, weight_z])
    return (cos_x, sin_x, cos_y, sin_y, forward_z, inverse_z, adjoint_z, spectrum_scale)


def rotate_half(values):
    middle = values.shape[-1] // 2
    return jnp.concatenate([values[..., middle:], -values[..., :middle]], -1)


def along_y(values, cosines, sine_table, inverse):
    pattern = "xjck,yj->xyck" if inverse else "xyck,yj->xjck"
    factor = -1.0 if inverse else 1.0
    direct = jnp.einsum(pattern, values, cosines)
    turned = jnp.einsum(pattern, rotate_half(values), sine_table)
    return direct + factor * turned


def along_x(values, cosines, sine_table, inverse):
    pattern = "jbck,xj->xbck" if inverse else "xbck,xj->jbck"
    factor = -1.0 if inverse else 1.0
    direct = jnp.einsum(pattern, values, cosines)
    turned = jnp.einsum(pattern, rotate_half(values), sine_table)
    return direct + factor * turned


def z_forward(field_in, matrix):
    shape_in = field_in.shape
    product = jnp.dot(
        field_in.reshape(-1, shape_in[-1]), matrix, preferred_element_type=jnp.float32
    )
    return product.reshape(shape_in[:-1] + (matrix.shape[1],))


def z_back(values, matrix):
    shape_in = values.shape
    product = jnp.dot(values.reshape(-1, shape_in[-1]), matrix, preferred_element_type=jnp.float32)
    return product.reshape(shape_in[:-1] + (matrix.shape[1],))


def gelu_slope(pre):
    normal_cdf = 0.5 * (1.0 + lax.erf(pre * (1.0 / math.sqrt(2.0))))
    return normal_cdf + pre * jnp.exp(-0.5 * pre * pre) * (1.0 / math.sqrt(2.0 * math.pi))


def apply_modes(coeffs, weights):
    real_part = coeffs[..., :MZ]
    imag_part = coeffs[..., MZ:]
    from_real = jnp.einsum(
        "sabik,abkio->sabok", real_part, weights, preferred_element_type=jnp.float32
    )
    from_imag = jnp.einsum(
        "sabik,abkio->sabok", imag_part, weights, preferred_element_type=jnp.float32
    )
    out_real = from_real[:, :, :, :CH] - from_imag[:, :, :, CH:]
    out_imag = from_real[:, :, :, CH:] + from_imag[:, :, :, :CH]
    return jnp.concatenate([out_real, out_imag], -1)


def paired(g_modes):
    g_real = g_modes[..., :MZ]
    g_imag = g_modes[..., MZ:]
    return (jnp.concatenate([g_real, g_imag], -2), jnp.concatenate([g_imag, -g_real], -2))


def adjoint_modes(g_modes, weights):
    paired_one, paired_two = paired(g_modes)
    back_real = jnp.einsum(
        "abkio,sabok->sabik", weights, paired_one, preferred_element_type=jnp.float32
    )
    back_imag = jnp.einsum(
        "abkio,sabok->sabik", weights, paired_two, preferred_element_type=jnp.float32
    )
    return jnp.concatenate([back_real, back_imag], -1)


def mode_grads(u_modes, g_modes):
    paired_one, paired_two = paired(g_modes)
    from_real = jnp.einsum(
        "sabik,sabok->abkio", u_modes[..., :MZ], paired_one, preferred_element_type=jnp.float32
    )
    from_imag = jnp.einsum(
        "sabik,sabok->abkio", u_modes[..., MZ:], paired_two, preferred_element_type=jnp.float32
    )
    return from_real + from_imag


def to_modes(field_in, tables):
    cos_x, sin_x, cos_y, sin_y, forward_z = (tables[0], tables[1], tables[2], tables[3], tables[4])
    sectioned = along_y(z_forward(field_in, forward_z), cos_y, sin_y, False)
    arrived = lax.all_to_all(
        sectioned.astype(jnp.bfloat16), "pencil", split_axis=1, concat_axis=0, tiled=True
    ).astype(sectioned.dtype)
    return along_x(arrived, cos_x, sin_x, False)


def to_grid(coeffs, tables, matrix):
    cos_x, sin_x, cos_y, sin_y = (tables[0], tables[1], tables[2], tables[3])
    sectioned = along_x(coeffs, cos_x, sin_x, True)
    arrived = lax.all_to_all(
        sectioned.astype(jnp.bfloat16), "pencil", split_axis=0, concat_axis=1, tiled=True
    ).astype(sectioned.dtype)
    return z_back(along_y(arrived, cos_y, sin_y, True), matrix)


def to_owner(coeffs):
    return lax.all_to_all(coeffs[None], "dp", split_axis=1, concat_axis=0, tiled=True)


def from_owner(coeffs):
    return lax.all_to_all(
        coeffs.astype(jnp.bfloat16), "dp", split_axis=0, concat_axis=1, tiled=True
    ).astype(coeffs.dtype)[0]


def body(field, cotangent, w_spec, w_local):
    tables = grid_tables()
    inverse_z, adjoint_z, spectrum_scale = (tables[5], tables[6], tables[7])
    sample = field[0]
    target = cotangent[0]
    u_modes = to_modes(sample, tables).astype(jnp.bfloat16)
    u_sent = to_owner(u_modes)
    v_modes = from_owner(apply_modes(u_sent, w_spec))
    values = to_grid(v_modes, tables, inverse_z)
    bypass = jnp.einsum("xycz,co->xyoz", sample, w_local, preferred_element_type=jnp.float32)
    slope_in = (target.astype(jnp.float32) * gelu_slope(values + bypass)).astype(jnp.bfloat16)
    g_modes = (to_modes(slope_in, tables) * spectrum_scale).astype(jnp.bfloat16)
    g_sent = to_owner(g_modes)
    grad_w = mode_grads(u_sent, g_sent)
    back_modes = from_owner(adjoint_modes(g_sent, w_spec))
    spread = jnp.einsum("xyoz,co->xycz", slope_in, w_local, preferred_element_type=jnp.float32)
    grad_sample = (to_grid(back_modes, tables, adjoint_z) + spread).astype(jnp.bfloat16)
    return (grad_sample[None], grad_w)


def solution(mesh):
    placed = (
        P("dp", "pencil", None, None, None),
        P("dp", "pencil", None, None, None),
        P("dp", "pencil", None, None, None),
        P(),
    )
    return jax.shard_map(
        body,
        mesh=mesh,
        in_specs=placed,
        out_specs=(P("dp", "pencil", None, None, None), P("dp", "pencil", None, None, None)),
        check_vma=False,
    )
```

profile of v0, /device:TPU:1, one launch (start us, length us, event | category | flops | bytes accessed | tf_op | source)
XLA Modules:
  0.0 167.1 jit_solution(9578072925121026040)
XLA Ops:
  0.7 3.7 %convolution_bitcast_fusion = f32[16384,32]{0,1:T(8,128)S(1)} fusion(bf16[16384,128]{1,0:T(8,128)(2,1)} %bitcast.246, bf16[128,16]{0,1:T(8,128)(2,1)S(1)} %get-tuple-element.21, bf16[128,16]{0,1:T(8,128)(2,1)S(1)} %get-tuple-element.22), kind=kOutput, calls=%fused_computation | convolution fusion | flops 134234112 | bytes 6299648 | tf_op jit(solution)/shard_map/dot_general | solution.py:64
  4.4 3.0 %reshape.248 = f32[4,64,64,32]{2,1,0,3:T(8,128)} reshape(f32[16384,32]{0,1:T(8,128)S(1)} %convolution_bitcast_fusion) | data formatting | bytes 4194304 | tf_op jit(solution)/shard_map/reshape | solution.py:67
  7.5 3.0 %fusion.229 = (bf16[4,64,64,16]{2,1,3,0:T(8,128)(2,1)S(1)}, bf16[4,64,64,16]{2,1,3,0:T(8,128)(2,1)S(1)}) fusion(f32[4,64,64,32]{2,1,0,3:T(8,128)} %reshape.248), kind=kLoop, calls=%fused_computation.258 | loop fusion | flops 524288 | bytes 4194304 | tf_op jit(solution)/shard_map/slice | solution.py:43
  12.6 20.5 %all_to_all.108 = bf16[16,2,4096]{2,1,0:T(2,128)(2,1)S(1)} all-to-all(bf16[16,2,4096]{2,1,0:T(2,128)(2,1)S(1)} %reshape.276), channel_id=1, replica_groups=mesh['dp'=16,'pencil'=16] {'pencil'}, dimensions={0} | all-to-all | bytes 524288 | tf_op jit(solution)/shard_map/all_to_all | solution.py:126
  35.4 9.0 %all-to-all-start.1 = ((bf16[16,2,1024]{2,1,0:T(2,128)(2,1)}), bf16[16,2,1024]{2,1,0:T(2,128)(2,1)S(1)}, u32[]{:S(2)}, u32[]{:S(2)}) async-start(bf16[16,2,1024]{2,1,0:T(2,128)(2,1)} %reshape.278), calls=%async_computation.1 | async-start | bytes 131072 | tf_op jit(solution)/shard_map/all_to_all | solution.py:142
  44.4 7.4 %all-to-all-done.1 = bf16[16,2,1024]{2,1,0:T(2,128)(2,1)S(1)} async-done(((bf16[16,2,1024]{2,1,0:T(2,128)(2,1)}), bf16[16,2,1024]{2,1,0:T(2,128)(2,1)S(1)}, u32[]{:S(2)}, u32[]{:S(2)}) %all-to-all-start.1) | async-done | bytes 65568 | tf_op jit(solution)/shard_map/all_to_all | solution.py:142
  53.4 3.7 %all-to-all-start.2 = ((bf16[16,2,1024]{2,1,0:T(2,128)(2,1)}), bf16[16,2,1024]{2,1,0:T(2,128)(2,1)S(1)}, u32[]{:S(2)}, u32[]{:S(2)}) async-start(bf16[16,2,1024]{2,1,0:T(2,128)(2,1)} %reshape.280), calls=%async_computation.2 | async-start | bytes 131072 | tf_op jit(solution)/shard_map/all_to_all | solution.py:146
  57.2 7.4 %all-to-all-done.2 = bf16[16,2,1024]{2,1,0:T(2,128)(2,1)S(1)} async-done(((bf16[16,2,1024]{2,1,0:T(2,128)(2,1)}), bf16[16,2,1024]{2,1,0:T(2,128)(2,1)S(1)}, u32[]{:S(2)}, u32[]{:S(2)}) %all-to-all-start.2) | async-done | bytes 65568 | tf_op jit(solution)/shard_map/all_to_all | solution.py:146
  67.1 3.7 %all-to-all-start.3 = ((bf16[16,2,4096]{2,1,0:T(2,128)(2,1)}), bf16[16,2,4096]{2,1,0:T(2,128)(2,1)S(1)}, u32[]{:S(2)}, u32[]{:S(2)}) async-start(bf16[16,2,4096]{2,1,0:T(2,128)(2,1)} %reshape.282), calls=%async_computation.3 | async-start | bytes 524288 | tf_op jit(solution)/shard_map/all_to_all | solution.py:135
  70.8 6.7 %fusion.12 = f32[64,4,64,128]{3,0,2,1:T(8,128)} fusion(bf16[1,4,64,64,128]{4,3,2,1,0:T(8,128)(2,1)} %param.4, bf16[64,64]{1,0:T(8,128)(2,1)S(1)} %copy-done.5), kind=kOutput, calls=%fused_computation.17 | convolution fusion | flops 268435456 | bytes 12591104 | tf_op jit(solution)/shard_map/xycz,co->xyoz/dot_general | solution.py:160
  77.6 4.4 %all-to-all-done.3 = bf16[16,2,4096]{2,1,0:T(2,128)(2,1)S(1)} async-done(((bf16[16,2,4096]{2,1,0:T(2,128)(2,1)}), bf16[16,2,4096]{2,1,0:T(2,128)(2,1)S(1)}, u32[]{:S(2)}, u32[]{:S(2)}) %all-to-all-start.3) | async-done | bytes 262176 | tf_op jit(solution)/shard_map/all_to_all | solution.py:135
  84.5 2.7 %copy-done.4 = f32[64,4,64,128]{3,0,2,1:T(8,128)S(1)} copy-done((f32[64,4,64,128]{3,0,2,1:T(8,128)S(1)}, f32[64,4,64,128]{3,0,2,1:T(8,128)}, u32[]{:S(2)}) %copy-start.4) | copy-done | bytes 8388632
  87.2 5.5 %fusion.5 = bf16[4,64,64,128]{3,2,1,0:T(8,128)(2,1)S(1)} fusion(f32[64,4,64,128]{3,0,2,1:T(8,128)S(1)} %copy-done.4, bf16[1,4,64,64,128]{4,3,2,1,0:T(8,128)(2,1)S(1)} %copy-done.6, bf16[4,64,64,32]{2,1,3,0:T(8,128)(2,1)S(1)} %add_bitcast_fusion.1, bf16[128,16]{0,1:T(8,128)(2,1)S(1)} %get-tuple-element.20, bf16[128,16]{0,1:T(8,128)(2,1)S(1)} %get-tuple-element.19), kind=kOutput, calls=%fused_computation.7 | convolution fusion | flops 159399936 | bytes 17833984 | tf_op jit(solution)/shard_map/dot_general | solution.py:72
  92.7 4.0 %fusion.101 = f32[4,64,64,32]{2,3,1,0:T(8,128)S(1)} fusion(bf16[4,64,64,128]{3,2,1,0:T(8,128)(2,1)S(1)} %fusion.5, bf16[128,16]{0,1:T(8,128)(2,1)S(1)} %get-tuple-element.21, bf16[128,16]{0,1:T(8,128)(2,1)S(1)} %get-tuple-element.22), kind=kOutput, calls=%fused_computation.141 | convolution fusion | flops 134234112 | bytes 6299648 | tf_op jit(solution)/shard_map/dot_general | solution.py:64
  98.3 2.4 %fusion.41 = bf16[4,16,64,32]{2,1,3,0:T(8,128)(2,1)S(1)} fusion(f32[16,4,64,32]{2,0,3,1:T(8,128)S(1)} %fusion.16, f32[4,64,64,32]{2,3,1,0:T(8,128)S(1)} %fusion.101, s32[16]{0:T(128)S(1)} %compare_select_fusion), kind=kOutput, calls=%fused_computation.45 | convolution fusion | flops 17053696 | bytes 2883648 | tf_op jit(solution)/shard_map/xyck,yj->xjck/dot_general | solution.py:49
  101.9 3.8 %all-to-all-start.4 = ((bf16[16,2,4096]{2,1,0:T(2,128)(2,1)}), bf16[16,2,4096]{2,1,0:T(2,128)(2,1)S(1)}, u32[]{:S(2)}, u32[]{:S(2)}) async-start(bf16[16,2,4096]{2,1,0:T(2,128)(2,1)} %reshape.284), calls=%async_computation.4 | async-start | bytes 524288 | tf_op jit(solution)/shard_map/all_to_all | solution.py:126
  105.8 9.6 %all-to-all-done.4 = bf16[16,2,4096]{2,1,0:T(2,128)(2,1)S(1)} async-done(((bf16[16,2,4096]{2,1,0:T(2,128)(2,1)}), bf16[16,2,4096]{2,1,0:T(2,128)(2,1)S(1)}, u32[]{:S(2)}, u32[]{:S(2)}) %all-to-all-start.4) | async-done | bytes 262176 | tf_op jit(solution)/shard_map/all_to_all | solution.py:126
  117.1 13.4 %all_to_all.109 = bf16[16,2,1024]{2,1,0:T(2,128)(2,1)S(1)} all-to-all(bf16[16,2,1024]{2,1,0:T(2,128)(2,1)S(1)} %reshape.286), channel_id=1, replica_groups=mesh['dp'=16,'pencil'=16] {'dp'}, dimensions={0} | all-to-all | bytes 131072 | tf_op jit(solution)/shard_map/all_to_all | solution.py:142
  131.5 10.2 %all_to_all.110 = bf16[16,2,1024]{2,1,0:T(2,128)(2,1)S(1)} all-to-all(bf16[16,2,1024]{2,1,0:T(2,128)(2,1)S(1)} %reshape.288), channel_id=1, replica_groups=mesh['dp'=16,'pencil'=16] {'dp'}, dimensions={0} | all-to-all | bytes 131072 | tf_op jit(solution)/shard_map/all_to_all | solution.py:146
  144.3 3.5 %all-to-all-start.7 = ((bf16[16,2,4096]{2,1,0:T(2,128)(2,1)}), bf16[16,2,4096]{2,1,0:T(2,128)(2,1)S(1)}, u32[]{:S(2)}, u32[]{:S(2)}) async-start(bf16[16,2,4096]{2,1,0:T(2,128)(2,1)} %reshape.290), calls=%async_computation.7 | async-start | bytes 524288 | tf_op jit(solution)/shard_map/all_to_all | solution.py:135
  148.2 1.1 fusion.40
  149.3 9.8 %all-to-all-done.7 = bf16[16,2,4096]{2,1,0:T(2,128)(2,1)S(1)} async-done(((bf16[16,2,4096]{2,1,0:T(2,128)(2,1)}), bf16[16,2,4096]{2,1,0:T(2,128)(2,1)S(1)}, u32[]{:S(2)}, u32[]{:S(2)}) %all-to-all-start.7) | async-done | bytes 262176 | tf_op jit(solution)/shard_map/all_to_all | solution.py:135
  161.7 2.2 %fusion.14 = f32[4,64,64,128]{3,2,1,0:T(8,128)S(1)} fusion(bf16[4,64,64,32]{2,1,3,0:T(8,128)(2,1)S(1)} %add_bitcast_fusion, bf16[128,16]{0,1:T(8,128)(2,1)S(1)} %get-tuple-element.21, bf16[128,16]{0,1:T(8,128)(2,1)S(1)} %get-tuple-element.22), kind=kOutput, calls=%fused_computation.19 | convolution fusion | flops 134234112 | bytes 9445376 | tf_op jit(solution)/shard_map/dot_general | solution.py:72
  163.9 3.2 %fusion.7 = bf16[1,4,64,64,128]{4,3,2,1,0:T(8,128)(2,1)} fusion(f32[4,64,64,128]{3,2,1,0:T(8,128)S(1)} %fusion.14, bf16[4,64,64,128]{3,2,1,0:T(8,128)(2,1)S(1)} %copy-done.2, bf16[64,64]{1,0:T(8,128)(2,1)S(1)} %copy-done.5), kind=kOutput, calls=%fused_computation.11 | convolution fusion | flops 272629760 | bytes 16785408 | tf_op jit(solution)/shard_map/xyoz,co->xycz/dot_general | solution.py:166
  (88 shorter events, 22.0 us)
Async XLA Ops:
  0.6 51.4 %copy-start = (bf16[1,1,16,64,128]{4,3,2,1,0:T(8,128)(2,1)S(1)}, bf16[1,1,16,64,128]{4,3,2,1,0:T(8,128)(2,1)}, u32[]{:S(2)}) copy-start(bf16[1,1,16,64,128]{4,3,2,1,0:T(8,128)(2,1)} %param.6) | copy-start | bytes 786436
  7.5 3.4 %copy-start.3 = (f32[4,64,64,32]{2,1,0,3:T(8,128)S(1)}, f32[4,64,64,32]{2,1,0,3:T(8,128)}, u32[]{:S(2)}) copy-start(f32[4,64,64,32]{2,1,0,3:T(8,128)} %reshape.248) | copy-start | bytes 6291460
  35.4 16.4 %all-to-all-start.1 = ((bf16[16,2,1024]{2,1,0:T(2,128)(2,1)}), bf16[16,2,1024]{2,1,0:T(2,128)(2,1)S(1)}, u32[]{:S(2)}, u32[]{:S(2)}) async-start(bf16[16,2,1024]{2,1,0:T(2,128)(2,1)} %reshape.278), calls=%async_computation.1 | async-start | bytes 131072 | tf_op jit(solution)/shard_map/all_to_all | solution.py:142
  52.0 18.8 %copy-start.5 = (bf16[64,64]{1,0:T(8,128)(2,1)S(1)}, bf16[64,64]{1,0:T(8,128)(2,1)}, u32[]{:S(2)}) copy-start(bf16[64,64]{1,0:T(8,128)(2,1)} %param.7) | copy-start | bytes 24580
  53.4 11.1 %all-to-all-start.2 = ((bf16[16,2,1024]{2,1,0:T(2,128)(2,1)}), bf16[16,2,1024]{2,1,0:T(2,128)(2,1)S(1)}, u32[]{:S(2)}, u32[]{:S(2)}) async-start(bf16[16,2,1024]{2,1,0:T(2,128)(2,1)} %reshape.280), calls=%async_computation.2 | async-start | bytes 131072 | tf_op jit(solution)/shard_map/all_to_all | solution.py:146
  67.1 14.8 %all-to-all-start.3 = ((bf16[16,2,4096]{2,1,0:T(2,128)(2,1)}), bf16[16,2,4096]{2,1,0:T(2,128)(2,1)S(1)}, u32[]{:S(2)}, u32[]{:S(2)}) async-start(bf16[16,2,4096]{2,1,0:T(2,128)(2,1)} %reshape.282), calls=%async_computation.3 | async-start | bytes 524288 | tf_op jit(solution)/shard_map/all_to_all | solution.py:135
  82.3 2.2 %copy-start.6 = (bf16[1,4,64,64,128]{4,3,2,1,0:T(8,128)(2,1)S(1)}, bf16[1,4,64,64,128]{4,3,2,1,0:T(8,128)(2,1)}, u32[]{:S(2)}) copy-start(bf16[1,4,64,64,128]{4,3,2,1,0:T(8,128)(2,1)} %param.5) | copy-start | bytes 12582916
  83.2 4.0 %copy-start.4 = (f32[64,4,64,128]{3,0,2,1:T(8,128)S(1)}, f32[64,4,64,128]{3,0,2,1:T(8,128)}, u32[]{:S(2)}) copy-start(f32[64,4,64,128]{3,0,2,1:T(8,128)} %fusion.12) | copy-start | bytes 25165828
  92.7 4.1 %copy-start.1 = (bf16[4,64,64,128]{3,2,1,0:T(8,128)(2,1)}, bf16[4,64,64,128]{3,2,1,0:T(8,128)(2,1)S(1)}, u32[]{:S(2)}) copy-start(bf16[4,64,64,128]{3,2,1,0:T(8,128)(2,1)S(1)} %fusion.5) | copy-start | bytes 12582916
  101.9 13.4 %all-to-all-start.4 = ((bf16[16,2,4096]{2,1,0:T(2,128)(2,1)}), bf16[16,2,4096]{2,1,0:T(2,128)(2,1)S(1)}, u32[]{:S(2)}, u32[]{:S(2)}) async-start(bf16[16,2,4096]{2,1,0:T(2,128)(2,1)} %reshape.284), calls=%async_computation.4 | async-start | bytes 524288 | tf_op jit(solution)/shard_map/all_to_all | solution.py:126
  144.3 14.8 %all-to-all-start.7 = ((bf16[16,2,4096]{2,1,0:T(2,128)(2,1)}), bf16[16,2,4096]{2,1,0:T(2,128)(2,1)S(1)}, u32[]{:S(2)}, u32[]{:S(2)}) async-start(bf16[16,2,4096]{2,1,0:T(2,128)(2,1)} %reshape.290), calls=%async_computation.7 | async-start | bytes 524288 | tf_op jit(solution)/shard_map/all_to_all | solution.py:135
  161.6 2.2 %copy-start.2 = (bf16[4,64,64,128]{3,2,1,0:T(8,128)(2,1)S(1)}, bf16[4,64,64,128]{3,2,1,0:T(8,128)(2,1)}, u32[]{:S(2)}) copy-start(bf16[4,64,64,128]{3,2,1,0:T(8,128)(2,1)} %copy-done.1) | copy-start | bytes 12582916
where the time goes:
time: 168 us; the launch traced here: 167 us
  blocking collectives  44.1 us (26%)
  matrix products  38.7 us (23%)
  waiting for transfers between devices  38.5 us (23%)
  starting transfers between devices  23.7 us (14%)
  local copies, waits for them, and re-layouts  15.3 us (9%)
  other arithmetic  5.77 us (3%)
    all_to_all x1, blocking collectives, to_modes(): lax.all_to_all(sectioned.astype(jnp.bfloat16), 'pencil', split_axis=1, co...  20.5 us
    all_to_all x2, waiting for transfers between devices, to_grid(): lax.all_to_all(sectioned.astype(jnp.bfloat16), 'pencil', split_axis=0, co...  14.2 us
    all_to_all x1, blocking collectives, to_owner(): lax.all_to_all(coeffs[None], 'dp', split_axis=1, concat_axis=0, tiled=True)  13.4 us
    unnamed x32, local copies, waits for them, and re-layouts  10.8 us
    all_to_all x1, blocking collectives, from_owner(): lax.all_to_all(coeffs.astype(jnp.bfloat16), 'dp', split_axis=0, concat_ax...  10.2 us
    all_to_all x1, waiting for transfers between devices, to_modes(): lax.all_to_all(sectioned.astype(jnp.bfloat16), 'pencil', split_axis=1, co...  9.57 us
    all_to_all x1, starting transfers between devices, to_owner(): lax.all_to_all(coeffs[None], 'dp', split_axis=1, concat_axis=0, tiled=True)  9.02 us
    dot_general x2, matrix products, z_forward(): jnp.dot(field_in.reshape(-1, shape_in[-1]), matrix, preferred_element_typ...  7.76 us
  transfers between devices with their start and end apart: 5, of which 5 were waited for; matrix products, arithmetic and copies ran while one was open for 5% of the time, Pallas kernels for 0%

commit v1 on v0

--- a/solution.py
+++ b/solution.py
@@ -139,7 +139,16 @@
 
 
 def to_owner(coeffs):
-    return lax.all_to_all(coeffs[None], "dp", split_axis=1, concat_axis=0, tiled=True)
+
+    def derive_the_spot(message, row_axis):
+        return jnp.concatenate(
+            lax.all_to_all(
+                jnp.stack(jnp.split(message, lax.psum(1, row_axis), axis=1), axis=0), row_axis, 0, 0
+            ),
+            axis=0,
+        )
+
+    return derive_the_spot(coeffs[None], "dp")
 
 
 def from_owner(coeffs):

time: 168 us -> 169 us (level)
    unnamed x32 -> x62, local copies, waits for them, and re-layouts: 10.8 us -> 11.1 us
where the time goes in v1:
time: 169 us; the launch traced here: 168 us
  blocking collectives  44.1 us (26%)
  matrix products  38.7 us (23%)
  waiting for transfers between devices  38.5 us (23%)
  starting transfers between devices  23.7 us (14%)
  local copies, waits for them, and re-layouts  16 us (9%)
  other arithmetic  5.77 us (3%)
    all_to_all x1, blocking collectives, to_modes(): lax.all_to_all(sectioned.astype(jnp.bfloat16), 'pencil', split_axis=1, co...  20.5 us
    all_to_all x2, waiting for transfers between devices, to_grid(): lax.all_to_all(sectioned.astype(jnp.bfloat16), 'pencil', split_axis=0, co...  14.2 us
    all_to_all x1, blocking collectives, derive_the_spot(): lax.all_to_all(jnp.stack(jnp.split(message, lax.psum(1, row_axis), axis=1...  13.3 us
    unnamed x62, local copies, waits for them, and re-layouts  11.1 us
    all_to_all x1, blocking collectives, from_owner(): lax.all_to_all(coeffs.astype(jnp.bfloat16), 'dp', split_axis=0, concat_ax...  10.2 us
    all_to_all x1, waiting for transfers between devices, to_modes(): lax.all_to_all(sectioned.astype(jnp.bfloat16), 'pencil', split_axis=1, co...  9.58 us
    all_to_all x1, starting transfers between devices, derive_the_spot(): lax.all_to_all(jnp.stack(jnp.split(message, lax.psum(1, row_axis), axis=1...  9.02 us
    dot_general x2, matrix products, z_forward(): jnp.dot(field_in.reshape(-1, shape_in[-1]), matrix, preferred_element_typ...  7.76 us
  transfers between devices with their start and end apart: 5, of which 5 were waited for; matrix products, arithmetic and copies ran while one was open for 5% of the time, Pallas kernels for 0%

profile of v1, /device:TPU:1, one launch (start us, length us, event | category | flops | bytes accessed | tf_op | source)
XLA Modules:
  0.0 168.1 jit_solution(4288391240555731905)
XLA Ops:
  0.7 3.7 %convolution_bitcast_fusion = f32[16384,32]{0,1:T(8,128)S(1)} fusion(bf16[16384,128]{1,0:T(8,128)(2,1)} %bitcast.306, bf16[128,16]{0,1:T(8,128)(2,1)S(1)} %get-tuple-element.53, bf16[128,16]{0,1:T(8,128)(2,1)S(1)} %get-tuple-element.54), kind=kOutput, calls=%fused_computation | convolution fusion | flops 134234112 | bytes 6299648 | tf_op jit(solution)/shard_map/dot_general | solution.py:64
  4.4 3.0 %reshape.248 = f32[4,64,64,32]{2,1,0,3:T(8,128)} reshape(f32[16384,32]{0,1:T(8,128)S(1)} %convolution_bitcast_fusion) | data formatting | bytes 4194304 | tf_op jit(solution)/shard_map/reshape | solution.py:67
  7.5 3.0 %fusion.229 = (bf16[4,64,64,16]{2,1,3,0:T(8,128)(2,1)S(1)}, bf16[4,64,64,16]{2,1,3,0:T(8,128)(2,1)S(1)}) fusion(f32[4,64,64,32]{2,1,0,3:T(8,128)} %reshape.248), kind=kLoop, calls=%fused_computation.290 | loop fusion | flops 524288 | bytes 4194304 | tf_op jit(solution)/shard_map/slice | solution.py:43
  12.6 20.5 %all_to_all.94 = bf16[16,2,4096]{2,1,0:T(2,128)(2,1)S(1)} all-to-all(bf16[16,2,4096]{2,1,0:T(2,128)(2,1)S(1)} %reshape.278), channel_id=1, replica_groups=mesh['dp'=16,'pencil'=16] {'pencil'}, dimensions={0} | all-to-all | bytes 524288 | tf_op jit(solution)/shard_map/all_to_all | solution.py:126
  35.9 9.0 %all-to-all-start.1 = ((bf16[16,2,1024]{2,1,0:T(2,128)(2,1)}), bf16[16,2,1024]{2,1,0:T(2,128)(2,1)S(1)}, u32[]{:S(2)}, u32[]{:S(2)}) async-start(bf16[16,2,1024]{2,1,0:T(2,128)(2,1)} %reshape.280), calls=%async_computation.1 | async-start | bytes 131072 | tf_op jit(solution)/shard_map/all_to_all | solution.py:145
  44.9 7.4 %all-to-all-done.1 = bf16[16,2,1024]{2,1,0:T(2,128)(2,1)S(1)} async-done(((bf16[16,2,1024]{2,1,0:T(2,128)(2,1)}), bf16[16,2,1024]{2,1,0:T(2,128)(2,1)S(1)}, u32[]{:S(2)}, u32[]{:S(2)}) %all-to-all-start.1) | async-done | bytes 65568 | tf_op jit(solution)/shard_map/all_to_all | solution.py:145
  53.9 3.7 %all-to-all-start.2 = ((bf16[16,2,1024]{2,1,0:T(2,128)(2,1)}), bf16[16,2,1024]{2,1,0:T(2,128)(2,1)S(1)}, u32[]{:S(2)}, u32[]{:S(2)}) async-start(bf16[16,2,1024]{2,1,0:T(2,128)(2,1)} %reshape.282), calls=%async_computation.2 | async-start | bytes 131072 | tf_op jit(solution)/shard_map/all_to_all | solution.py:155
  57.6 7.4 %all-to-all-done.2 = bf16[16,2,1024]{2,1,0:T(2,128)(2,1)S(1)} async-done(((bf16[16,2,1024]{2,1,0:T(2,128)(2,1)}), bf16[16,2,1024]{2,1,0:T(2,128)(2,1)S(1)}, u32[]{:S(2)}, u32[]{:S(2)}) %all-to-all-start.2) | async-done | bytes 65568 | tf_op jit(solution)/shard_map/all_to_all | solution.py:155
  67.6 3.7 %all-to-all-start.3 = ((bf16[16,2,4096]{2,1,0:T(2,128)(2,1)}), bf16[16,2,4096]{2,1,0:T(2,128)(2,1)S(1)}, u32[]{:S(2)}, u32[]{:S(2)}) async-start(bf16[16,2,4096]{2,1,0:T(2,128)(2,1)} %reshape.284), calls=%async_computation.3 | async-start | bytes 524288 | tf_op jit(solution)/shard_map/all_to_all | solution.py:135
  71.3 6.8 %fusion.12 = f32[64,4,64,128]{3,0,2,1:T(8,128)} fusion(bf16[1,4,64,64,128]{4,3,2,1,0:T(8,128)(2,1)} %param.4, bf16[64,64]{1,0:T(8,128)(2,1)S(1)} %copy-done.5), kind=kOutput, calls=%fused_computation.17 | convolution fusion | flops 268435456 | bytes 12591104 | tf_op jit(solution)/shard_map/xycz,co->xyoz/dot_general | solution.py:169
  78.1 4.3 %all-to-all-done.3 = bf16[16,2,4096]{2,1,0:T(2,128)(2,1)S(1)} async-done(((bf16[16,2,4096]{2,1,0:T(2,128)(2,1)}), bf16[16,2,4096]{2,1,0:T(2,128)(2,1)S(1)}, u32[]{:S(2)}, u32[]{:S(2)}) %all-to-all-start.3) | async-done | bytes 262176 | tf_op jit(solution)/shard_map/all_to_all | solution.py:135
  85.0 2.7 %copy-done.4 = f32[64,4,64,128]{3,0,2,1:T(8,128)S(1)} copy-done((f32[64,4,64,128]{3,0,2,1:T(8,128)S(1)}, f32[64,4,64,128]{3,0,2,1:T(8,128)}, u32[]{:S(2)}) %copy-start.4) | copy-done | bytes 8388632
  87.7 5.5 %fusion.5 = bf16[4,64,64,128]{3,2,1,0:T(8,128)(2,1)S(1)} fusion(f32[64,4,64,128]{3,0,2,1:T(8,128)S(1)} %copy-done.4, bf16[1,4,64,64,128]{4,3,2,1,0:T(8,128)(2,1)S(1)} %copy-done.6, bf16[4,64,64,32]{2,1,3,0:T(8,128)(2,1)S(1)} %add_bitcast_fusion.1, bf16[128,16]{0,1:T(8,128)(2,1)S(1)} %get-tuple-element.52, bf16[128,16]{0,1:T(8,128)(2,1)S(1)} %get-tuple-element.51), kind=kOutput, calls=%fused_computation.7 | convolution fusion | flops 159399936 | bytes 17833984 | tf_op jit(solution)/shard_map/dot_general | solution.py:72
  93.1 4.0 %fusion.101 = f32[4,64,64,32]{2,3,1,0:T(8,128)S(1)} fusion(bf16[4,64,64,128]{3,2,1,0:T(8,128)(2,1)S(1)} %fusion.5, bf16[128,16]{0,1:T(8,128)(2,1)S(1)} %get-tuple-element.53, bf16[128,16]{0,1:T(8,128)(2,1)S(1)} %get-tuple-element.54), kind=kOutput, calls=%fused_computation.173 | convolution fusion | flops 134234112 | bytes 6299648 | tf_op jit(solution)/shard_map/dot_general | solution.py:64
  98.7 2.4 %fusion.41 = bf16[4,16,64,32]{2,1,3,0:T(8,128)(2,1)S(1)} fusion(f32[16,4,64,32]{2,0,3,1:T(8,128)S(1)} %fusion.16, f32[4,64,64,32]{2,3,1,0:T(8,128)S(1)} %fusion.101, s32[16]{0:T(128)S(1)} %compare_select_fusion), kind=kOutput, calls=%fused_computation.45 | convolution fusion | flops 17053696 | bytes 2883648 | tf_op jit(solution)/shard_map/xyck,yj->xjck/dot_general | solution.py:49
  102.4 3.8 %all-to-all-start.4 = ((bf16[16,2,4096]{2,1,0:T(2,128)(2,1)}), bf16[16,2,4096]{2,1,0:T(2,128)(2,1)S(1)}, u32[]{:S(2)}, u32[]{:S(2)}) async-start(bf16[16,2,4096]{2,1,0:T(2,128)(2,1)} %reshape.286), calls=%async_computation.4 | async-start | bytes 524288 | tf_op jit(solution)/shard_map/all_to_all | solution.py:126
  106.2 9.6 %all-to-all-done.4 = bf16[16,2,4096]{2,1,0:T(2,128)(2,1)S(1)} async-done(((bf16[16,2,4096]{2,1,0:T(2,128)(2,1)}), bf16[16,2,4096]{2,1,0:T(2,128)(2,1)S(1)}, u32[]{:S(2)}, u32[]{:S(2)}) %all-to-all-start.4) | async-done | bytes 262176 | tf_op jit(solution)/shard_map/all_to_all | solution.py:126
  118.0 13.3 %all_to_all.95 = bf16[16,2,1024]{2,1,0:T(2,128)(2,1)S(1)} all-to-all(bf16[16,2,1024]{2,1,0:T(2,128)(2,1)S(1)} %reshape.288), channel_id=1, replica_groups=mesh['dp'=16,'pencil'=16] {'dp'}, dimensions={0} | all-to-all | bytes 131072 | tf_op jit(solution)/shard_map/all_to_all | solution.py:145
  132.4 10.2 %all_to_all.96 = bf16[16,2,1024]{2,1,0:T(2,128)(2,1)S(1)} all-to-all(bf16[16,2,1024]{2,1,0:T(2,128)(2,1)S(1)} %reshape.290), channel_id=1, replica_groups=mesh['dp'=16,'pencil'=16] {'dp'}, dimensions={0} | all-to-all | bytes 131072 | tf_op jit(solution)/shard_map/all_to_all | solution.py:155
  145.3 3.5 %all-to-all-start.7 = ((bf16[16,2,4096]{2,1,0:T(2,128)(2,1)}), bf16[16,2,4096]{2,1,0:T(2,128)(2,1)S(1)}, u32[]{:S(2)}, u32[]{:S(2)}) async-start(bf16[16,2,4096]{2,1,0:T(2,128)(2,1)} %reshape.292), calls=%async_computation.7 | async-start | bytes 524288 | tf_op jit(solution)/shard_map/all_to_all | solution.py:135
  149.1 1.1 fusion.40
  150.2 9.8 %all-to-all-done.7 = bf16[16,2,4096]{2,1,0:T(2,128)(2,1)S(1)} async-done(((bf16[16,2,4096]{2,1,0:T(2,128)(2,1)}), bf16[16,2,4096]{2,1,0:T(2,128)(2,1)S(1)}, u32[]{:S(2)}, u32[]{:S(2)}) %all-to-all-start.7) | async-done | bytes 262176 | tf_op jit(solution)/shard_map/all_to_all | solution.py:135
  162.6 2.2 %fusion.14 = f32[4,64,64,128]{3,2,1,0:T(8,128)S(1)} fusion(bf16[4,64,64,32]{2,1,3,0:T(8,128)(2,1)S(1)} %add_bitcast_fusion, bf16[128,16]{0,1:T(8,128)(2,1)S(1)} %get-tuple-element.53, bf16[128,16]{0,1:T(8,128)(2,1)S(1)} %get-tuple-element.54), kind=kOutput, calls=%fused_computation.19 | convolution fusion | flops 134234112 | bytes 9445376 | tf_op jit(solution)/shard_map/dot_general | solution.py:72
  164.8 3.3 %fusion.7 = bf16[1,4,64,64,128]{4,3,2,1,0:T(8,128)(2,1)} fusion(f32[4,64,64,128]{3,2,1,0:T(8,128)S(1)} %fusion.14, bf16[4,64,64,128]{3,2,1,0:T(8,128)(2,1)S(1)} %copy-done.2, bf16[64,64]{1,0:T(8,128)(2,1)S(1)} %copy-done.5), kind=kOutput, calls=%fused_computation.11 | convolution fusion | flops 272629760 | bytes 16785408 | tf_op jit(solution)/shard_map/xyoz,co->xycz/dot_general | solution.py:175
  (120 shorter events, 22.9 us)
Async XLA Ops:
  0.6 51.8 %copy-start = (bf16[1,1,16,64,128]{4,3,2,1,0:T(8,128)(2,1)S(1)}, bf16[1,1,16,64,128]{4,3,2,1,0:T(8,128)(2,1)}, u32[]{:S(2)}) copy-start(bf16[1,1,16,64,128]{4,3,2,1,0:T(8,128)(2,1)} %param.6) | copy-start | bytes 786436
  7.5 3.4 %copy-start.3 = (f32[4,64,64,32]{2,1,0,3:T(8,128)S(1)}, f32[4,64,64,32]{2,1,0,3:T(8,128)}, u32[]{:S(2)}) copy-start(f32[4,64,64,32]{2,1,0,3:T(8,128)} %reshape.248) | copy-start | bytes 6291460
  35.9 16.4 %all-to-all-start.1 = ((bf16[16,2,1024]{2,1,0:T(2,128)(2,1)}), bf16[16,2,1024]{2,1,0:T(2,128)(2,1)S(1)}, u32[]{:S(2)}, u32[]{:S(2)}) async-start(bf16[16,2,1024]{2,1,0:T(2,128)(2,1)} %reshape.280), calls=%async_computation.1 | async-start | bytes 131072 | tf_op jit(solution)/shard_map/all_to_all | solution.py:145
  52.5 18.8 %copy-start.5 = (bf16[64,64]{1,0:T(8,128)(2,1)S(1)}, bf16[64,64]{1,0:T(8,128)(2,1)}, u32[]{:S(2)}) copy-start(bf16[64,64]{1,0:T(8,128)(2,1)} %param.7) | copy-start | bytes 24580
  53.9 11.1 %all-to-all-start.2 = ((bf16[16,2,1024]{2,1,0:T(2,128)(2,1)}), bf16[16,2,1024]{2,1,0:T(2,128)(2,1)S(1)}, u32[]{:S(2)}, u32[]{:S(2)}) async-start(bf16[16,2,1024]{2,1,0:T(2,128)(2,1)} %reshape.282), calls=%async_computation.2 | async-start | bytes 131072 | tf_op jit(solution)/shard_map/all_to_all | solution.py:155
  67.6 14.8 %all-to-all-start.3 = ((bf16[16,2,4096]{2,1,0:T(2,128)(2,1)}), bf16[16,2,4096]{2,1,0:T(2,128)(2,1)S(1)}, u32[]{:S(2)}, u32[]{:S(2)}) async-start(bf16[16,2,4096]{2,1,0:T(2,128)(2,1)} %reshape.284), calls=%async_computation.3 | async-start | bytes 524288 | tf_op jit(solution)/shard_map/all_to_all | solution.py:135
  82.8 2.2 %copy-start.6 = (bf16[1,4,64,64,128]{4,3,2,1,0:T(8,128)(2,1)S(1)}, bf16[1,4,64,64,128]{4,3,2,1,0:T(8,128)(2,1)}, u32[]{:S(2)}) copy-start(bf16[1,4,64,64,128]{4,3,2,1,0:T(8,128)(2,1)} %param.5) | copy-start | bytes 12582916
  83.7 4.0 %copy-start.4 = (f32[64,4,64,128]{3,0,2,1:T(8,128)S(1)}, f32[64,4,64,128]{3,0,2,1:T(8,128)}, u32[]{:S(2)}) copy-start(f32[64,4,64,128]{3,0,2,1:T(8,128)} %fusion.12) | copy-start | bytes 25165828
  93.1 4.1 %copy-start.1 = (bf16[4,64,64,128]{3,2,1,0:T(8,128)(2,1)}, bf16[4,64,64,128]{3,2,1,0:T(8,128)(2,1)S(1)}, u32[]{:S(2)}) copy-start(bf16[4,64,64,128]{3,2,1,0:T(8,128)(2,1)S(1)} %fusion.5) | copy-start | bytes 12582916
  102.4 13.4 %all-to-all-start.4 = ((bf16[16,2,4096]{2,1,0:T(2,128)(2,1)}), bf16[16,2,4096]{2,1,0:T(2,128)(2,1)S(1)}, u32[]{:S(2)}, u32[]{:S(2)}) async-start(bf16[16,2,4096]{2,1,0:T(2,128)(2,1)} %reshape.286), calls=%async_computation.4 | async-start | bytes 524288 | tf_op jit(solution)/shard_map/all_to_all | solution.py:126
  145.3 14.8 %all-to-all-start.7 = ((bf16[16,2,4096]{2,1,0:T(2,128)(2,1)}), bf16[16,2,4096]{2,1,0:T(2,128)(2,1)S(1)}, u32[]{:S(2)}, u32[]{:S(2)}) async-start(bf16[16,2,4096]{2,1,0:T(2,128)(2,1)} %reshape.292), calls=%async_computation.7 | async-start | bytes 524288 | tf_op jit(solution)/shard_map/all_to_all | solution.py:135
  162.6 2.2 %copy-start.2 = (bf16[4,64,64,128]{3,2,1,0:T(8,128)(2,1)S(1)}, bf16[4,64,64,128]{3,2,1,0:T(8,128)(2,1)}, u32[]{:S(2)}) copy-start(bf16[4,64,64,128]{3,2,1,0:T(8,128)(2,1)} %copy-done.1) | copy-start | bytes 12582916
